TPU v7x, 8 devices: a whole 2x2x1 slice. The times are simulated.
8 devices in a mesh: dp: 1 (over z), tp: 2 (over y), sp: 4 (over x, core).
Axes of the slice: x: 2, y: 2, z: 1, core: 2. Of those that a mesh axis runs over, the one named last changes fastest.
Arguments:
- step_emb: bfloat16 [4, 32, 1024], P(None, 'dp')
- v_cache: bfloat16 [2, 32, 1024, 1024], P(None, 'dp', 'sp', 'tp')
- z_cache: bfloat16 [2, 32, 1024, 1024], P(None, 'dp', 'sp', 'tp')
- short_state: bfloat16 [2, 32, 2, 3, 1024], P(None, 'dp', None, None, 'tp')
- w_in: bfloat16 [2, 1024, 3, 1024], P(None, None, None, 'tp')
- b_in: float32 [2, 3, 1024], P(None, None, 'tp')
- short_taps: float32 [2, 3, 3, 1024], P(None, None, None, 'tp')
- long_filt: float32 [2, 2, 1024, 1024], P(None, None, None, 'tp')
- skip_gain: float32 [2, 2, 1024], P(None, None, 'tp')
- w_out: bfloat16 [2, 1024, 1024], P(None, 'tp')
- b_out: float32 [2, 1024], replicated
- w_up: bfloat16 [2, 1024, 4096], P(None, None, 'tp')
- w_down: bfloat16 [2, 4096, 1024], P(None, 'tp')
Outputs:
- output 1: float32 [4, 32, 1024], P(None, 'dp')
- output 2: bfloat16 [2, 32, 1024, 1024], P(None, 'dp', 'sp', 'tp')
- output 3: bfloat16 [2, 32, 1024, 1024], P(None, 'dp', 'sp', 'tp')
- output 4: bfloat16 [2, 32, 2, 3, 1024], P(None, 'dp', None, None, 'tp')
All inputs are finite; a program needn't handle non-finite values.
Results may differ from a plain program's by a relative error of at most 0.0117668.
Values sent between devices are 32-bit elements.
A program may use at most 1 GiB of HBM per device.

v0:
```python
import jax
import jax.numpy as jnp
from jax import lax
from jax.sharding import PartitionSpec as P

NUM_STEPS = 4
NUM_LAYERS = 2


def layer_norm(rows_in):
    mean_val = jnp.mean(rows_in, axis=-1, keepdims=True)
    centered = rows_in - mean_val
    var_val = jnp.mean(centered * centered, axis=-1, keepdims=True)
    return centered * lax.rsqrt(var_val + 1e-5)


def filter_windows(long_filt, shard_start, start_pos, shard_len):
    lag_pos = start_pos + 3 - shard_start - jnp.arange(shard_len + 3)
    picked = jnp.take(long_filt, jnp.maximum(lag_pos, 0), axis=2)
    return jnp.where((lag_pos >= 0)[:, None], picked, 0.0)


def append_row(cache_all, layer_idx, new_row, local_pos):
    num_seq = cache_all.shape[1]
    shard_len = cache_all.shape[2]
    chan_dim = cache_all.shape[3]
    inside = (local_pos >= 0) & (local_pos < shard_len)
    row_slot = jnp.clip(local_pos, 0, shard_len - 1)
    old_row = lax.dynamic_slice(cache_all, (layer_idx, 0, row_slot, 0), (1, num_seq, 1, chan_dim))
    put_row = jnp.where(inside, new_row[None, :, None, :], old_row)
    return lax.dynamic_update_slice(cache_all, put_row, (layer_idx, 0, row_slot, 0))


def solution(mesh):
    sp_size = mesh.shape["sp"]

    def device_fn(step_emb, v_cache, z_cache, short_state, w_in, b_in, short_taps, long_filt, skip_gain, w_out, b_out, w_up, w_down):
        shard_len = v_cache.shape[2]
        start_pos = shard_len * sp_size * 3 // 4
        shard_start = lax.axis_index("sp") * shard_len
        windows = filter_windows(long_filt, shard_start, start_pos, shard_len)
        v_all = v_cache
        z_all = z_cache
        states = [short_state[layer_idx] for layer_idx in range(NUM_LAYERS)]
        hidden_rows = []
        for step_idx in range(NUM_STEPS):
            local_pos = start_pos + step_idx - shard_start
            win_start = 3 - step_idx
            hidden = step_emb[step_idx].astype(jnp.float32)
            for layer_idx in range(NUM_LAYERS):
                normed = layer_norm(hidden).astype(jnp.bfloat16)
                proj_row = jnp.einsum("bd,dgc->bgc", normed, w_in[layer_idx], preferred_element_type=jnp.float32)
                proj_row = (proj_row + b_in[layer_idx]).astype(jnp.bfloat16)
                prev_state = states[layer_idx]
                tap_rows = short_taps[layer_idx]
                mixed_rows = (tap_rows[0] * proj_row.astype(jnp.float32)
                              + tap_rows[1] * prev_state[:, 1].astype(jnp.float32)
                              + tap_rows[2] * prev_state[:, 0].astype(jnp.float32))
                states[layer_idx] = jnp.stack([prev_state[:, 1], proj_row], axis=1)
                value_row = mixed_rows[:, 2].astype(jnp.bfloat16)
                v_all = append_row(v_all, layer_idx, value_row, local_pos)
                part_one = jnp.sum(v_all[layer_idx] * windows[layer_idx, 0, win_start:win_start + shard_len][None], axis=1)
                long_one = lax.psum(part_one, "sp") + skip_gain[layer_idx, 0] * value_row.astype(jnp.float32)
                z_row = (mixed_rows[:, 0] * long_one).astype(jnp.bfloat16)
                z_all = append_row(z_all, layer_idx, z_row, local_pos)
                part_two = jnp.sum(z_all[layer_idx] * windows[layer_idx, 1, win_start:win_start + shard_len][None], axis=1)
                long_two = lax.psum(part_two, "sp") + skip_gain[layer_idx, 1] * z_row.astype(jnp.float32)
                y_row = (mixed_rows[:, 1] * long_two).astype(jnp.bfloat16)
                mix_out = lax.psum(jnp.dot(y_row, w_out[layer_idx], preferred_element_type=jnp.float32), "tp")
                hidden = hidden + mix_out + b_out[layer_idx]
                inner_act = jax.nn.gelu(jnp.dot(layer_norm(hidden).astype(jnp.bfloat16), w_up[layer_idx], preferred_element_type=jnp.float32)).astype(jnp.bfloat16)
                hidden = hidden + lax.psum(jnp.dot(inner_act, w_down[layer_idx], preferred_element_type=jnp.float32), "tp")
            hidden_rows.append(hidden)
        return (jnp.stack(hidden_rows), v_all, z_all, jnp.stack(states))

    specs_in = (
        P(None, "dp", None),
        P(None, "dp", "sp", "tp"),
        P(None, "dp", "sp", "tp"),
        P(None, "dp", None, None, "tp"),
        P(None, None, None, "tp"),
        P(None, None, "tp"),
        P(None, None, None, "tp"),
        P(None, None, None, "tp"),
        P(None, None, "tp"),
        P(None, "tp", None),
        P(None, None),
        P(None, None, "tp"),
        P(None, "tp", None),
    )
    specs_out = (
        P(None, "dp", None),
        P(None, "dp", "sp", "tp"),
        P(None, "dp", "sp", "tp"),
        P(None, "dp", None, None, "tp"),
    )
    return jax.shard_map(device_fn, mesh=mesh, in_specs=specs_in, out_specs=specs_out, check_vma=False)
```

profile of v0, /device:TPU:0, one launch (start us, length us, event | category | flops | bytes accessed | tf_op | source)
XLA Modules:
  0.0 746.3 jit_solution(11958784339004921120)
XLA Ops:
  14.2 18.5 %copy.28 = bf16[2,32,256,512]{3,1,2,0:T(8,128)(2,1)} copy(bf16[2,32,256,512]{3,2,1,0:T(8,128)(2,1)} %param.14) | data formatting | bytes 33554432 | tf_op args[1]
  32.7 13.7 %gather_fusion = f32[259,2,2,512]{3,0,2,1:T(8,128)S(1)} fusion(f32[2,2,1024,512]{3,2,1,0:T(8,128)} %param.20, s32[1024]{0:T(1024)S(1)} %pad_clamp_fusion), kind=kCustom, calls=%fused_computation | custom fusion | bytes 4244492 | tf_op jit(solution)/shard_map/jit(_take)/gather | solution.py:19
  55.2 6.0 fusion.15
  62.1 18.5 %copy.30 = bf16[2,32,256,512]{3,1,2,0:T(8,128)(2,1)} copy(bf16[2,32,256,512]{3,2,1,0:T(8,128)(2,1)} %param.15) | data formatting | bytes 33554432 | tf_op args[2]
  80.6 9.6 %all-reduce.27.cloned.1.call-done = f32[32,512]{1,0:T(8,128)} async-done(((f32[32,512]{1,0:T(8,128)}), f32[32,512]{1,0:T(8,128)}) %all-reduce.27.cloned.1.call-update) | async-done | bytes 65552 | tf_op jit(solution)/shard_map/psum | solution.py:63
  91.7 6.0 fusion.14
  99.6 24.2 %all-reduce.29.cloned.1.call-done = f32[32,512]{1,0:T(8,128)} async-done(((f32[32,512]{1,0:T(8,128)}), f32[32,512]{1,0:T(8,128)}) %all-reduce.29.cloned.1.call-update) | async-done | bytes 65552 | tf_op jit(solution)/shard_map/psum | solution.py:67
  126.3 15.6 %all-reduce.31.cloned.1.call-done = f32[32,1024]{1,0:T(8,128)} async-done(((f32[32,1024]{1,0:T(8,128)}), f32[32,1024]{1,0:T(8,128)}) %all-reduce.31.cloned.1.call-update) | async-done | bytes 131088 | tf_op jit(solution)/shard_map/psum | solution.py:69
  145.7 5.8 fusion.38
  155.6 11.9 %all-reduce.33.cloned.1.call-done = f32[32,1024]{1,0:T(8,128)} async-done(((f32[32,1024]{1,0:T(8,128)}), f32[32,1024]{1,0:T(8,128)}) %all-reduce.33.cloned.1.call-update) | async-done | bytes 131088 | tf_op jit(solution)/shard_map/psum | solution.py:72
  174.6 6.0 fusion.13
  182.1 6.3 fusion.11
  188.9 26.0 %all-reduce.61.cloned.1.call-done = (f32[32,512]{1,0:T(8,128)}, f32[32,512]{1,0:T(8,128)}) async-done(((f32[32,512]{1,0:T(8,128)}, f32[32,512]{1,0:T(8,128)}), (f32[32,512]{1,0:T(8,128)}, f32[32,512]{1,0:T(8,128)})) %all-reduce.61.cloned.1.call-update) | async-done | bytes 131088 | tf_op jit(solution)/shard_map/psum | solution.py:63
  216.5 6.0 fusion.12
  224.0 6.4 fusion.10
  230.5 26.0 %all-reduce.35.cloned.1.call-done = f32[32,512]{1,0:T(8,128)} async-done(((f32[32,512]{1,0:T(8,128)}), f32[32,512]{1,0:T(8,128)}) %all-reduce.35.cloned.1.call-update) | async-done | bytes 65552 | tf_op jit(solution)/shard_map/psum | solution.py:67
  259.6 15.6 %all-reduce.37.cloned.1.call-done = f32[32,1024]{1,0:T(8,128)} async-done(((f32[32,1024]{1,0:T(8,128)}), f32[32,1024]{1,0:T(8,128)}) %all-reduce.37.cloned.1.call-update) | async-done | bytes 131088 | tf_op jit(solution)/shard_map/psum | solution.py:69
  277.3 5.8 fusion.36
  286.7 12.4 %all-reduce.39.cloned.1.call-done = f32[32,1024]{1,0:T(8,128)} async-done(((f32[32,1024]{1,0:T(8,128)}), f32[32,1024]{1,0:T(8,128)}) %all-reduce.39.cloned.1.call-update) | async-done | bytes 131088 | tf_op jit(solution)/shard_map/psum | solution.py:72
  305.9 6.0 fusion.9
  313.4 6.3 fusion.7
  320.0 26.2 %all-reduce.59.cloned.1.call-done = (f32[32,512]{1,0:T(8,128)}, f32[32,512]{1,0:T(8,128)}) async-done(((f32[32,512]{1,0:T(8,128)}, f32[32,512]{1,0:T(8,128)}), (f32[32,512]{1,0:T(8,128)}, f32[32,512]{1,0:T(8,128)})) %all-reduce.59.cloned.1.call-update) | async-done | bytes 131088 | tf_op jit(solution)/shard_map/psum | solution.py:63
  347.9 6.0 fusion.8
  355.3 6.3 fusion.6
  361.7 26.0 %all-reduce.41.cloned.1.call-done = f32[32,512]{1,0:T(8,128)} async-done(((f32[32,512]{1,0:T(8,128)}), f32[32,512]{1,0:T(8,128)}) %all-reduce.41.cloned.1.call-update) | async-done | bytes 65552 | tf_op jit(solution)/shard_map/psum | solution.py:67
  389.6 16.2 %all-reduce.43.cloned.1.call-done = f32[32,1024]{1,0:T(8,128)} async-done(((f32[32,1024]{1,0:T(8,128)}), f32[32,1024]{1,0:T(8,128)}) %all-reduce.43.cloned.1.call-update) | async-done | bytes 131088 | tf_op jit(solution)/shard_map/psum | solution.py:69
  409.7 5.8 fusion.34
  419.0 12.5 %all-reduce.45.cloned.1.call-done = f32[32,1024]{1,0:T(8,128)} async-done(((f32[32,1024]{1,0:T(8,128)}), f32[32,1024]{1,0:T(8,128)}) %all-reduce.45.cloned.1.call-update) | async-done | bytes 131088 | tf_op jit(solution)/shard_map/psum | solution.py:72
  438.7 6.0 fusion.5
  446.2 6.3 fusion.3
  452.8 26.2 %all-reduce.57.cloned.1.call-done = (f32[32,512]{1,0:T(8,128)}, f32[32,512]{1,0:T(8,128)}) async-done(((f32[32,512]{1,0:T(8,128)}, f32[32,512]{1,0:T(8,128)}), (f32[32,512]{1,0:T(8,128)}, f32[32,512]{1,0:T(8,128)})) %all-reduce.57.cloned.1.call-update) | async-done | bytes 131088 | tf_op jit(solution)/shard_map/psum | solution.py:63
  480.6 6.0 fusion.4
  488.1 6.3 fusion.2
  494.5 26.0 %all-reduce.47.cloned.1.call-done = f32[32,512]{1,0:T(8,128)} async-done(((f32[32,512]{1,0:T(8,128)}), f32[32,512]{1,0:T(8,128)}) %all-reduce.47.cloned.1.call-update) | async-done | bytes 65552 | tf_op jit(solution)/shard_map/psum | solution.py:67
  522.4 16.6 %all-reduce.49.cloned.1.call-done = f32[32,1024]{1,0:T(8,128)} async-done(((f32[32,1024]{1,0:T(8,128)}), f32[32,1024]{1,0:T(8,128)}) %all-reduce.49.cloned.1.call-update) | async-done | bytes 131088 | tf_op jit(solution)/shard_map/psum | solution.py:69
  542.3 5.8 fusion.32
  548.1 15.9 %all-reduce.51.cloned.1.call-done = f32[32,1024]{1,0:T(8,128)} async-done(((f32[32,1024]{1,0:T(8,128)}), f32[32,1024]{1,0:T(8,128)}) %all-reduce.51.cloned.1.call-update) | async-done | bytes 131088 | tf_op jit(solution)/shard_map/psum | solution.py:72
  570.4 6.0 fusion.1
  576.6 26.0 %all-reduce.53.cloned.1.call-done = f32[32,512]{1,0:T(8,128)} async-done(((f32[32,512]{1,0:T(8,128)}), f32[32,512]{1,0:T(8,128)}) %all-reduce.53.cloned.1.call-update) | async-done | bytes 65552 | tf_op jit(solution)/shard_map/psum | solution.py:63
  604.1 6.0 fusion
  610.2 26.9 %all-reduce.55.cloned.1.call-done = (f32[32,512]{1,0:T(8,128)}, f32[32,512]{1,0:T(8,128)}, f32[32,512]{1,0:T(8,128)}, f32[32,512]{1,0:T(8,128)}) async-done(((f32[32,512]{1,0:T(8,128)}, f32[32,512]{1,0:T(8,128)}, f32[32,512]{1,0:T(8,128)}, f32[32,512]{1,0:T(8,128)}), (f32[32,512]{1,0:T(8,128)}, f32[32,512]{1,0:T(8,128)}, f32[32,512]{1,0:T(8,128)}, f32[32,512]{1,0:T(8,128)})) %all-reduce.55.cloned.1.call-update) | async-done | bytes 262160 | tf_op jit(solution)/shard_map/psum | solution.py:67
  644.7 22.7 %all-reduce.65.cloned.1.call-done = (f32[32,1024]{1,0:T(8,128)}, f32[32,1024]{1,0:T(8,128)}, f32[32,1024]{1,0:T(8,128)}, f32[32,1024]{1,0:T(8,128)}) async-done(((f32[32,1024]{1,0:T(8,128)}, f32[32,1024]{1,0:T(8,128)}, f32[32,1024]{1,0:T(8,128)}, f32[32,1024]{1,0:T(8,128)}), (f32[32,1024]{1,0:T(8,128)}, f32[32,1024]{1,0:T(8,128)}, f32[32,1024]{1,0:T(8,128)}, ...) | async-done | bytes 524304 | tf_op jit(solution)/shard_map/psum | solution.py:69
  669.0 5.7 fusion.22
  674.9 5.7 fusion.20
  680.8 5.7 fusion.18
  686.8 5.7 fusion.16
  692.6 19.5 %copy.32 = bf16[2,32,256,512]{3,2,1,0:T(8,128)(2,1)} copy(bf16[2,32,256,512]{3,1,2,0:T(8,128)(2,1)} %fusion.475) | data formatting | bytes 33554432
  713.3 21.2 %copy.33 = bf16[2,32,256,512]{3,2,1,0:T(8,128)(2,1)} copy(bf16[2,32,256,512]{3,1,2,0:T(8,128)(2,1)S(1)} %bitcast.705) | data formatting | bytes 33554432
  (269 shorter events, 112.8 us)
Async XLA Ops:
  7.2 83.0 %all-reduce.27.cloned.1.call-start = ((), (), s32[]{:S(2)}) async-start(), calls=%async_computation | async-start | bytes 131072 | tf_op jit(solution)/shard_map/psum | solution.py:63
  8.1 42.3 %copy-start.30 = (f32[1,1,3,512]{3,2,0,1:T(4,128)}, f32[1,1,3,512]{3,2,0,1:T(4,128)S(1)}, u32[]{:S(2)}) copy-start(f32[1,1,3,512]{3,2,0,1:T(4,128)S(1)} %copy.58) | copy-start | bytes 18436
  14.2 36.3 %copy-start.32 = (f32[1,3,512]{2,1,0:T(4,128)}, f32[1,3,512]{2,1,0:T(4,128)S(1)}, u32[]{:S(2)}) copy-start(f32[1,3,512]{2,1,0:T(4,128)S(1)} %copy.57) | copy-start | bytes 18436
  61.2 62.7 %all-reduce.29.cloned.1.call-start = ((), (), s32[]{:S(2)}) async-start(), calls=%async_computation.1 | async-start | bytes 131072 | tf_op jit(solution)/shard_map/psum | solution.py:67
  62.0 28.1 %copy-start.46 = (f32[1,1,512]{2,1,0:T(1,128)}, f32[1,1,512]{2,1,0:T(1,128)S(1)}, u32[]{:S(2)}) copy-start(f32[1,1,512]{2,1,0:T(1,128)S(1)} %get-tuple-element.100) | copy-start | bytes 6148
  62.1 61.8 %copy-start.45 = (f32[1,1,512]{2,1,0:T(1,128)}, f32[1,1,512]{2,1,0:T(1,128)S(1)}, u32[]{:S(2)}) copy-start(f32[1,1,512]{2,1,0:T(1,128)S(1)} %get-tuple-element.99) | copy-start | bytes 6148
  80.5 43.3 %copy-start = (bf16[2,512,1024]{2,1,0:T(8,128)(2,1)S(1)}, bf16[2,512,1024]{2,1,0:T(8,128)(2,1)}, u32[]{:S(2)}) copy-start(bf16[2,512,1024]{2,1,0:T(8,128)(2,1)} %param.22) | copy-start | bytes 6291460
  80.6 45.2 %copy-start.50 = (f32[2,1024]{1,0:T(2,128)S(1)}, f32[2,1024]{1,0:T(2,128)}, u32[]{:S(2)}) copy-start(f32[2,1024]{1,0:T(2,128)} %param.23) | copy-start | bytes 24580
  97.8 44.1 %all-reduce.31.cloned.1.call-start = ((), (), s32[]{:S(2)}) async-start(), calls=%async_computation.2 | async-start | bytes 262144 | tf_op jit(solution)/shard_map/psum | solution.py:69
  125.7 41.8 %all-reduce.33.cloned.1.call-start = ((), (), s32[]{:S(2)}) async-start(), calls=%async_computation.3 | async-start | bytes 262144 | tf_op jit(solution)/shard_map/psum | solution.py:72
  141.9 25.5 %copy-start.14 = (f32[32,1024]{1,0:T(8,128)S(1)}, f32[32,1024]{1,0:T(8,128)}, u32[]{:S(2)}) copy-start(f32[32,1024]{1,0:T(8,128)} %all-reduce.31.cloned.1.call-done) | copy-start | bytes 393220
  151.5 63.4 %all-reduce.61.cloned.1.call-start = ((), (), s32[]{:S(2)}) async-start(), calls=%async_computation.17 | async-start | bytes 262144 | tf_op jit(solution)/shard_map/psum | solution.py:63
  167.5 14.7 %copy-start.7 = (f32[256,512]{1,0:T(8,128)S(1)}, f32[256,512]{1,0:T(8,128)}, u32[]{:S(2)}) copy-start(f32[256,512]{1,0:T(8,128)} %get-tuple-element.84) | copy-start | bytes 1572868
  174.6 40.3 %copy-start.44 = (f32[1,1,512]{2,1,0:T(1,128)S(1)}, f32[1,1,512]{2,1,0:T(1,128)}, u32[]{:S(2)}) copy-start(f32[1,1,512]{2,1,0:T(1,128)} %get-tuple-element.101) | copy-start | bytes 6148
  182.1 40.5 %copy-start.47 = (f32[1,1,512]{2,1,0:T(1,128)S(1)}, f32[1,1,512]{2,1,0:T(1,128)}, u32[]{:S(2)}) copy-start(f32[1,1,512]{2,1,0:T(1,128)} %copy-done.46) | copy-start | bytes 6148
  188.5 68.0 %all-reduce.35.cloned.1.call-start = ((), (), s32[]{:S(2)}) async-start(), calls=%async_computation.4 | async-start | bytes 131072 | tf_op jit(solution)/shard_map/psum | solution.py:67
  224.0 59.2 %copy-start.31 = (f32[1,1,3,512]{3,2,0,1:T(4,128)S(1)}, f32[1,1,3,512]{3,2,0,1:T(4,128)}, u32[]{:S(2)}) copy-start(f32[1,1,3,512]{3,2,0,1:T(4,128)} %copy-done.30) | copy-start | bytes 18436
  224.0 59.2 %copy-start.33 = (f32[1,3,512]{2,1,0:T(4,128)S(1)}, f32[1,3,512]{2,1,0:T(4,128)}, u32[]{:S(2)}) copy-start(f32[1,3,512]{2,1,0:T(4,128)} %copy-done.32) | copy-start | bytes 18436
  224.0 59.2 %copy-start.35 = (f32[3,512]{1,0:T(4,128)S(1)}, f32[3,512]{1,0:T(4,128)}, u32[]{:S(2)}) copy-start(f32[3,512]{1,0:T(4,128)} %copy-done.34) | copy-start | bytes 18436
  224.0 59.2 %copy-start.37 = (f32[3,512]{1,0:T(4,128)S(1)}, f32[3,512]{1,0:T(4,128)}, u32[]{:S(2)}) copy-start(f32[3,512]{1,0:T(4,128)} %copy-done.36) | copy-start | bytes 18436
  230.4 44.7 %all-reduce.37.cloned.1.call-start = ((), (), s32[]{:S(2)}) async-start(), calls=%async_computation.5 | async-start | bytes 262144 | tf_op jit(solution)/shard_map/psum | solution.py:69
  258.3 40.8 %all-reduce.39.cloned.1.call-start = ((), (), s32[]{:S(2)}) async-start(), calls=%async_computation.6 | async-start | bytes 262144 | tf_op jit(solution)/shard_map/psum | solution.py:72
  283.1 63.1 %all-reduce.59.cloned.1.call-start = ((), (), s32[]{:S(2)}) async-start(), calls=%async_computation.16 | async-start | bytes 262144 | tf_op jit(solution)/shard_map/psum | solution.py:63
  319.8 68.0 %all-reduce.41.cloned.1.call-start = ((), (), s32[]{:S(2)}) async-start(), calls=%async_computation.7 | async-start | bytes 131072 | tf_op jit(solution)/shard_map/psum | solution.py:67
  361.7 44.1 %all-reduce.43.cloned.1.call-start = ((), (), s32[]{:S(2)}) async-start(), calls=%async_computation.8 | async-start | bytes 262144 | tf_op jit(solution)/shard_map/psum | solution.py:69
  389.6 41.9 %all-reduce.45.cloned.1.call-start = ((), (), s32[]{:S(2)}) async-start(), calls=%async_computation.9 | async-start | bytes 262144 | tf_op jit(solution)/shard_map/psum | solution.py:72
  415.5 63.4 %all-reduce.57.cloned.1.call-start = ((), (), s32[]{:S(2)}) async-start(), calls=%async_computation.15 | async-start | bytes 262144 | tf_op jit(solution)/shard_map/psum | solution.py:63
  431.5 14.7 %copy-start.3 = (f32[256,512]{1,0:T(8,128)S(1)}, f32[256,512]{1,0:T(8,128)}, u32[]{:S(2)}) copy-start(f32[256,512]{1,0:T(8,128)} %get-tuple-element.76) | copy-start | bytes 1572868
  452.6 68.0 %all-reduce.47.cloned.1.call-start = ((), (), s32[]{:S(2)}) async-start(), calls=%async_computation.10 | async-start | bytes 131072 | tf_op jit(solution)/shard_map/psum | solution.py:67
  494.4 44.6 %all-reduce.49.cloned.1.call-start = ((), (), s32[]{:S(2)}) async-start(), calls=%async_computation.11 | async-start | bytes 262144 | tf_op jit(solution)/shard_map/psum | solution.py:69
  522.4 41.6 %all-reduce.51.cloned.1.call-start = ((), (), s32[]{:S(2)}) async-start(), calls=%async_computation.12 | async-start | bytes 262144 | tf_op jit(solution)/shard_map/psum | solution.py:72
  548.1 54.5 %all-reduce.53.cloned.1.call-start = ((), (), s32[]{:S(2)}) async-start(), calls=%async_computation.13 | async-start | bytes 131072 | tf_op jit(solution)/shard_map/psum | solution.py:63
  576.4 60.7 %copy-start.38 = (bf16[32,512]{1,0:T(8,128)(2,1)S(1)}, bf16[32,512]{1,0:T(8,128)(2,1)}, u32[]{:S(2)}) copy-start(bf16[32,512]{1,0:T(8,128)(2,1)} %get-tuple-element.67) | copy-start | bytes 98308
  576.4 62.5 %copy-start.39 = (bf16[32,512]{1,0:T(8,128)(2,1)S(1)}, bf16[32,512]{1,0:T(8,128)(2,1)}, u32[]{:S(2)}) copy-start(bf16[32,512]{1,0:T(8,128)(2,1)} %get-tuple-element.61) | copy-start | bytes 98308
  576.4 64.3 %copy-start.40 = (bf16[32,512]{1,0:T(8,128)(2,1)S(1)}, bf16[32,512]{1,0:T(8,128)(2,1)}, u32[]{:S(2)}) copy-start(bf16[32,512]{1,0:T(8,128)(2,1)} %get-tuple-element.55) | copy-start | bytes 98308
  576.4 91.0 %copy-start.9 = (f32[32,1024]{1,0:T(8,128)S(1)}, f32[32,1024]{1,0:T(8,128)}, u32[]{:S(2)}) copy-start(f32[32,1024]{1,0:T(8,128)} %copy-done.8) | copy-start | bytes 393220
  576.5 91.0 %copy-start.11 = (f32[32,1024]{1,0:T(8,128)S(1)}, f32[32,1024]{1,0:T(8,128)}, u32[]{:S(2)}) copy-start(f32[32,1024]{1,0:T(8,128)} %copy-done.10) | copy-start | bytes 393220
  576.5 91.0 %copy-start.13 = (f32[32,1024]{1,0:T(8,128)S(1)}, f32[32,1024]{1,0:T(8,128)}, u32[]{:S(2)}) copy-start(f32[32,1024]{1,0:T(8,128)} %copy-done.12) | copy-start | bytes 393220
  576.5 91.0 %copy-start.48 = (f32[1,1024]{1,0:T(1,128)S(1)}, f32[1,1024]{1,0:T(1,128)}, u32[]{:S(2)}) copy-start(f32[1,1024]{1,0:T(1,128)} %get-tuple-element.103) | copy-start | bytes 12292
  576.5 60.6 %all-reduce.55.cloned.1.call-start = ((), (), s32[]{:S(2)}) async-start(), calls=%async_computation.14 | async-start | bytes 524288 | tf_op jit(solution)/shard_map/psum | solution.py:67
  610.2 57.3 %all-reduce.65.cloned.1.call-start = ((), (), s32[]{:S(2)}) async-start(), calls=%async_computation.19 | async-start | bytes 1048576 | tf_op jit(solution)/shard_map/psum | solution.py:69
  644.4 90.1 %all-reduce.63.cloned.1.call-start = ((), (), s32[]{:S(2)}) async-start(), calls=%async_computation.18 | async-start | bytes 1048576 | tf_op jit(solution)/shard_map/psum | solution.py:72
  692.5 20.8 %slice-start = ((s8[16777216]{0:T(1024)(128)(4,1)}), s8[4194304]{0:T(1024)(128)(4,1)S(1)}, s32[]{:S(2)}) async-start(s8[16777216]{0:T(1024)(128)(4,1)} %bitcast.704), calls=%async_computation.20 | async-start | bytes 8388608
  692.6 19.5 %copy-start.22 = (bf16[32,3,512]{2,0,1:T(8,128)(2,1)S(1)}, bf16[32,3,512]{2,0,1:T(8,128)(2,1)}, u32[]{:S(2)}) copy-start(bf16[32,3,512]{2,0,1:T(8,128)(2,1)} %get-tuple-element.123) | copy-start | bytes 294916
  692.6 19.5 %copy-start.27 = (bf16[32,3,512]{2,0,1:T(8,128)(2,1)S(1)}, bf16[32,3,512]{2,0,1:T(8,128)(2,1)}, u32[]{:S(2)}) copy-start(bf16[32,3,512]{2,0,1:T(8,128)(2,1)} %get-tuple-element.125) | copy-start | bytes 294916
  692.6 20.7 %slice-start.1 = ((s8[16777216]{0:T(1024)(128)(4,1)}), s8[4194304]{0:T(1024)(128)(4,1)S(1)}, s32[]{:S(2)}) async-start(s8[16777216]{0:T(1024)(128)(4,1)} %bitcast.704), calls=%async_computation.21 | async-start | bytes 8388608
  692.6 20.7 %slice-start.2 = ((s8[16777216]{0:T(1024)(128)(4,1)}), s8[4194304]{0:T(1024)(128)(4,1)S(1)}, s32[]{:S(2)}) async-start(s8[16777216]{0:T(1024)(128)(4,1)} %bitcast.704), calls=%async_computation.22 | async-start | bytes 8388608
  692.6 20.7 %slice-start.3 = ((s8[16777216]{0:T(1024)(128)(4,1)}), s8[4194304]{0:T(1024)(128)(4,1)S(1)}, s32[]{:S(2)}) async-start(s8[16777216]{0:T(1024)(128)(4,1)} %bitcast.704), calls=%async_computation.23 | async-start | bytes 8388608
  (30 other events, 184.2 us)
Sparse Core Ops, SparseCore 0:
  61.3 28.7 all-reduce.26
  97.9 25.9 all-reduce.28
  126.1 15.7 all-reduce.30
  151.6 15.7 all-reduce.32
  188.6 26.2 all-reduce.60
  230.5 25.9 all-reduce.34
  259.3 15.7 all-reduce.36
  283.2 15.8 all-reduce.38
  319.9 26.2 all-reduce.58
  361.8 25.9 all-reduce.40
  390.0 15.7 all-reduce.42
  415.7 15.7 all-reduce.44
  452.7 26.2 all-reduce.56
  494.6 25.9 all-reduce.46
  523.2 15.7 all-reduce.48
  548.2 15.7 all-reduce.50
  576.6 25.9 all-reduce.52
  610.3 26.8 all-reduce.54
  644.5 22.8 all-reduce.64
  692.6 22.8 all-reduce.62
where the time goes:
time: 756 us; the launch traced here: 746 us
  waiting for transfers between devices  383 us (51%)
  other arithmetic  151 us (20%)
  local copies, waits for them, and re-layouts  108 us (14%)
  matrix products  87.5 us (12%)
  between operations  15.3 us (2%)
    psum x5, waiting for transfers between devices, device_fn(): lax.psum(part_two, 'sp')  129 us
    psum x5, waiting for transfers between devices, device_fn(): lax.psum(part_one, 'sp')  114 us
    psum x5, waiting for transfers between devices, device_fn(): lax.psum(jnp.dot(y_row, w_out[layer_idx], preferred_element_type=jnp.floa...  86.7 us
    unnamed x127, local copies, waits for them, and re-layouts  85.8 us
    psum x5, waiting for transfers between devices, device_fn(): lax.psum(jnp.dot(inner_act, w_down[layer_idx], preferred_element_type=jnp...  52.7 us
    reduce_sum x8, other arithmetic, device_fn(): jnp.sum(z_all[layer_idx] * windows[layer_idx, 1, win_start:win_start + sh...  49.2 us
    reduce_sum x8, other arithmetic, device_fn(): jnp.sum(v_all[layer_idx] * windows[layer_idx, 0, win_start:win_start + sh...  49.1 us
    dot_general x8, matrix products, device_fn(): jnp.dot(inner_act, w_down[layer_idx], preferred_element_type=jnp.float32)  46 us
  transfers between devices with their start and end apart: 20, of which 19 were waited for; matrix products, arithmetic and copies ran while one was open for 10% of the time, Pallas kernels for 0%

commit v1 on v0

v1 whole, which is shorter than its diff:
```python
import functools

import jax
import jax.numpy as jnp
from jax import lax
from jax.experimental import pallas as pl
from jax.experimental.pallas import tpu as pltpu
from jax.sharding import PartitionSpec as P

F32 = jnp.float32
BF16 = jnp.bfloat16
NUM_STEPS = 4
NUM_LAYERS = 2
SEQ = 32
BLK = 8
DIM = 1024
CH = 512
UP = 2048
SHARD = 256
NCH = 2
CW = DIM // NCH
MESH = pl.DeviceIdType.MESH


def reduce_rows(accs):
    sub = lax.broadcasted_iota(jnp.int32, (8, 128), 0)
    low4 = sub < 4
    low2 = (sub % 4) < 2
    low1 = (sub % 2) < 1
    lev = [jnp.where(low4, accs[i], accs[i + 4]) + pltpu.roll(jnp.where(low4, accs[i + 4], accs[i]), 4, 0) for i in range(4)]
    lev = [jnp.where(low2, lev[i] + pltpu.roll(lev[i], 6, 0), lev[i + 2] + pltpu.roll(lev[i + 2], 2, 0)) for i in range(2)]
    return jnp.where(low1, lev[0] + pltpu.roll(lev[0], 7, 0), lev[1] + pltpu.roll(lev[1], 1, 0))


def conv_kernel(shard_ref, v_ref, z_ref, filt_ref, tail_ref, v_out, z_out, part_ref, win, sems):
    layer = pl.program_id(0)
    blk = pl.program_id(1)
    copies = []
    for idx, (src, dst) in enumerate(((v_ref, v_out), (z_ref, z_out))):
        copy = pltpu.make_async_copy(src.at[0], dst.at[layer, pl.ds(blk * BLK, BLK)], sems.at[idx])
        copy.start()
        copies.append(copy)

    @pl.when(blk == 0)
    def _():
        flip = 7 - lax.broadcasted_iota(jnp.int32, (8, CH), 0)
        for f in range(2):
            for j in range(NUM_STEPS):
                for m in range(SHARD // 8):
                    lo = SHARD + j - 8 * m - 7
                    if m == 0:
                        rows = jnp.concatenate([filt_ref[f, lo:SHARD, :], tail_ref[f, 0:j + 1, :]], axis=0)
                    else:
                        rows = filt_ref[f, lo:lo + 8, :]
                    win[f, j, 8 * m:8 * m + 8, :] = jnp.take_along_axis(rows, flip, axis=0)

    for f, src in enumerate((v_ref, z_ref)):
        for ct in range(CH // 128):
            lanes = slice(128 * ct, 128 * ct + 128)

            def body(pt, accs, f=f, src=src, lanes=lanes):
                base = pl.multiple_of(pt * 16, 16)
                w = [[win[f, j, pl.ds(base + 8 * h, 8), lanes] for h in range(2)] for j in range(NUM_STEPS)]
                out = []
                for b in range(BLK):
                    x = src[0, b, pl.ds(base, 16), lanes].astype(F32)
                    for j in range(NUM_STEPS):
                        out.append(accs[b * NUM_STEPS + j] + x[:8] * w[j][0] + x[8:] * w[j][1])
                return tuple(out)

            zero = jnp.zeros((8, 128), F32)
            accs = lax.fori_loop(0, SHARD // 16, body, (zero,) * (BLK * NUM_STEPS))
            for j in range(NUM_STEPS):
                part_ref[f, j, :, lanes] = reduce_rows([accs[b * NUM_STEPS + j] for b in range(BLK)])
    for copy in copies:
        copy.wait()


def conv_call(shard, v_cache, z_cache, long_filt):
    sq = pl.Squeezed()
    cache_spec = pl.BlockSpec((1, BLK, SHARD, CH), lambda l, b, s: (l, b, 0, 0))
    return pl.pallas_call(
        conv_kernel,
        out_shape=(
            jax.ShapeDtypeStruct(v_cache.shape, BF16),
            jax.ShapeDtypeStruct(z_cache.shape, BF16),
            jax.ShapeDtypeStruct((SEQ // BLK, NUM_LAYERS, 2, NUM_STEPS, BLK, CH), F32),
        ),
        grid_spec=pltpu.PrefetchScalarGridSpec(
            num_scalar_prefetch=1,
            grid=(NUM_LAYERS, SEQ // BLK),
            in_specs=[
                cache_spec,
                cache_spec,
                pl.BlockSpec((sq, 2, SHARD, CH), lambda l, b, s: (l, 0, jnp.maximum(2 - s[0], 0), 0)),
                pl.BlockSpec((sq, 2, 8, CH), lambda l, b, s: (l, 0, (jnp.maximum(2 - s[0], 0) + 1) * (SHARD // 8), 0)),
            ],
            out_specs=[
                pl.BlockSpec(memory_space=pl.ANY),
                pl.BlockSpec(memory_space=pl.ANY),
                pl.BlockSpec((sq, sq, 2, NUM_STEPS, BLK, CH), lambda l, b, s: (b, l, 0, 0, 0, 0)),
            ],
            scratch_shapes=[
                pltpu.VMEM((2, NUM_STEPS, SHARD, CH), F32),
                pltpu.SemaphoreType.DMA((2,)),
            ],
        ),
        compiler_params=pltpu.CompilerParams(dimension_semantics=("arbitrary", "arbitrary"), vmem_limit_bytes=60 << 20),
        name="conv_stream",
    )(shard, v_cache, z_cache, long_filt, long_filt)


def norm_rows(rows_in):
    mean_val = jnp.mean(rows_in, axis=-1, keepdims=True)
    centered = rows_in - mean_val
    var_val = jnp.mean(centered * centered, axis=-1, keepdims=True)
    return centered * lax.rsqrt(var_val + 1e-5)


def round_bf16(x):
    return x.astype(BF16).astype(F32)


def layer_kernel(part_ref, emb_ref, state_ref, b_in_ref, taps_ref, lag_ref, gain_ref, b_out_ref,
                 w_in_hbm, w_out_hbm, w_up_hbm, w_down_hbm,
                 hid_ref, st_ref, rows_ref,
                 w_in, w_out, w_up, w_down, emb32, p_all, rs_buf, x_send, x_recv, hid_buf, st_buf, row_buf,
                 w_sem, rs_send, rs_recv, x_ssem, x_rsem, st_ssem, st_rsem, row_ssem, row_rsem, g_ssem, g_rsem):
    k = lax.axis_index("sp")
    t = lax.axis_index("tp")
    others = [lax.rem(k + d, 4) for d in range(1, 4)]
    mate = k + 1 - 2 * lax.rem(k, 2)
    across = lax.rem(k + 2, 4)
    own = pl.ds(pl.multiple_of(k * BLK, BLK), BLK)

    w_copies = []
    for layer in range(NUM_LAYERS):
        for idx, (src, dst) in enumerate(((w_in_hbm, w_in), (w_out_hbm, w_out), (w_up_hbm, w_up), (w_down_hbm, w_down))):
            copy = pltpu.make_async_copy(src.at[layer], dst.at[layer], w_sem.at[layer, idx])
            copy.start()
            w_copies.append(copy)

    barrier = pltpu.get_barrier_semaphore()
    for dev in others:
        pl.semaphore_signal(barrier, inc=1, device_id={"sp": dev}, device_id_type=MESH)
    pl.semaphore_signal(barrier, inc=1, device_id={"tp": 1 - t}, device_id_type=MESH)
    pl.semaphore_wait(barrier, 4)

    def rs_copy(layer, f, d):
        dev = others[d]
        return pltpu.make_async_remote_copy(
            src_ref=part_ref.at[dev, layer, f], dst_ref=rs_buf.at[jnp.minimum(k, 2), layer, f],
            send_sem=rs_send.at[layer, f, d], recv_sem=rs_recv.at[layer, f, d],
            device_id={"sp": dev}, device_id_type=MESH)

    @pl.when(k < 3)
    def _():
        for layer in range(NUM_LAYERS):
            for f in range(2):
                for d in range(3):
                    rs_copy(layer, f, d).start()
        rs_buf[jnp.minimum(k, 2)] = part_ref[k]

    def cached_sum(layer, f):
        for d in range(3):
            @pl.when(lax.rem(k + 3 - d, 4) < 3)
            def _():
                rs_copy(layer, f, d).wait_recv()
        return (rs_buf[0, layer, f] + rs_buf[1, layer, f]) + rs_buf[2, layer, f]

    def tap_mix(layer, g, cur, prev1, prev2):
        return (taps_ref[layer, 0, g:g + 1] * cur + taps_ref[layer, 1, g:g + 1] * prev1
                + taps_ref[layer, 2, g:g + 1] * prev2)

    def x_copy(n, c):
        return pltpu.make_async_remote_copy(
            src_ref=x_send.at[n, c], dst_ref=x_recv.at[n, c], send_sem=x_ssem.at[n, c], recv_sem=x_rsem.at[n, c],
            device_id={"tp": 1 - t}, device_id_type=MESH)

    def row_copy(n, which, layer):
        piece = row_buf.at[which, layer, :, own]
        return pltpu.make_async_remote_copy(
            src_ref=piece, dst_ref=piece, send_sem=row_ssem.at[n], recv_sem=row_rsem.at[n, k],
            device_id={"sp": 3}, device_id_type=MESH)

    def send_rows(n, which, layer):
        @pl.when(k < 3)
        def _():
            row_copy(n, which, layer).start()

    def long_conv(layer, f, cached, vals):
        outs = []
        for j in range(NUM_STEPS):
            acc = cached[j]
            for i in range(j + 1):
                acc = acc + lag_ref[layer, f, j - i:j - i + 1] * vals[i]
            outs.append(acc + gain_ref[layer, f:f + 1] * vals[j])
        return outs

    def gates(layer, x1, x2, vals):
        a = long_conv(layer, 0, cached_sum(layer, 0), vals)
        z = [round_bf16(x1[j] * a[j]) for j in range(NUM_STEPS)]
        for j in range(NUM_STEPS):
            row_buf[1, layer, j, own] = z[j]
        send_rows(layer * 2, 1, layer)
        b = long_conv(layer, 1, cached_sum(layer, 1), z)
        return jnp.concatenate([x2[j] * b[j] for j in range(NUM_STEPS)], axis=0).astype(BF16)

    def matmul_exchange(n, lhs, w_ref):
        for c in range(NCH):
            x_send[n, c] = jnp.dot(lhs, w_ref[:, c * CW:(c + 1) * CW], preferred_element_type=F32)
            x_copy(n, c).start()

    def add_exchange(n, c, base):
        x_copy(n, c).wait_recv()
        return base + (x_send[n, c] + x_recv[n, c])

    def mlp(layer, mixed):
        act = norm_rows(mixed).astype(BF16)
        w_copies[layer * 4 + 2].wait()
        inner = jax.nn.gelu(jnp.dot(act, w_up[layer], preferred_element_type=F32)).astype(BF16)
        w_copies[layer * 4 + 3].wait()
        matmul_exchange(layer * 2 + 1, inner, w_down.at[layer])

    def mixed_rows(layer, rows_in):
        n = layer * 2
        return jnp.concatenate(
            [add_exchange(n, c, rows_in[:, c * CW:(c + 1) * CW]) + b_out_ref[layer:layer + 1, c * CW:(c + 1) * CW]
             for c in range(NCH)], axis=1)

    emb32[...] = emb_ref[...].astype(F32)
    normed = norm_rows(emb32[...].reshape(NUM_STEPS * SEQ, DIM)).astype(BF16)
    w_copies[0].wait()
    for g in range(3):
        proj = jnp.dot(normed, w_in[0, g], preferred_element_type=F32) + b_in_ref[0, g:g + 1]
        p_all[g] = round_bf16(proj).reshape(NUM_STEPS, SEQ, CH)

    def p0(g, j, rows):
        return p_all[g, j, rows] if j >= 0 else state_ref[0, j + 2, g, rows]

    everyone = slice(0, SEQ)
    for g in range(3):
        for s in range(2):
            st_ref[0, s, g] = p_all[g, 2 + s]
    for j in range(NUM_STEPS):
        row_buf[0, 0, j] = round_bf16(tap_mix(0, 2, *[p0(2, j - i, everyone) for i in range(3)]))
    x1 = [tap_mix(0, 0, *[p0(0, j - i, own) for i in range(3)]) for j in range(NUM_STEPS)]
    x2 = [tap_mix(0, 1, *[p0(1, j - i, own) for i in range(3)]) for j in range(NUM_STEPS)]
    y = gates(0, x1, x2, [row_buf[0, 0, j, own] for j in range(NUM_STEPS)])
    w_copies[1].wait()
    matmul_exchange(0, y, w_out.at[0])
    mixed = mixed_rows(0, jnp.concatenate([emb32[j, own] for j in range(NUM_STEPS)], axis=0))
    mlp(0, mixed)
    hidden = jnp.concatenate([add_exchange(1, c, mixed[:, c * CW:(c + 1) * CW]) for c in range(NCH)], axis=1)

    normed = norm_rows(hidden).astype(BF16)
    w_copies[4].wait()
    p1 = []
    for g in range(3):
        proj = round_bf16(jnp.dot(normed, w_in[1, g], preferred_element_type=F32) + b_in_ref[1, g:g + 1])
        p1.append([state_ref[1, 0, g, own], state_ref[1, 1, g, own]] + [proj[BLK * j:BLK * j + BLK] for j in range(NUM_STEPS)])
        for s in range(2):
            st_buf[s, g, own] = proj[BLK * (2 + s):BLK * (3 + s)]

    def st_copy(d):
        piece = st_buf.at[:, :, own]
        return pltpu.make_async_remote_copy(
            src_ref=piece, dst_ref=piece, send_sem=st_ssem.at[d], recv_sem=st_rsem.at[d],
            device_id={"sp": others[d]}, device_id_type=MESH)

    for d in range(3):
        st_copy(d).start()
    mix1 = [[tap_mix(1, g, p1[g][j + 2], p1[g][j + 1], p1[g][j]) for j in range(NUM_STEPS)] for g in range(3)]
    vals = [round_bf16(mix1[2][j]) for j in range(NUM_STEPS)]
    for j in range(NUM_STEPS):
        row_buf[0, 1, j, own] = vals[j]
    send_rows(1, 0, 1)
    y = gates(1, mix1[0], mix1[1], vals)
    w_copies[5].wait()
    matmul_exchange(2, y, w_out.at[1])
    mixed = mixed_rows(1, hidden)
    mlp(1, mixed)

    def g_copy(c, hop):
        block = k if hop < 2 else across
        dev = across if hop == 1 else mate
        piece = hid_buf.at[c, :, pl.ds(pl.multiple_of(block * BLK, BLK), BLK)]
        return pltpu.make_async_remote_copy(
            src_ref=piece, dst_ref=piece, send_sem=g_ssem.at[c, hop], recv_sem=g_rsem.at[c, hop],
            device_id={"sp": dev}, device_id_type=MESH)

    for c in range(NCH):
        done = add_exchange(3, c, mixed[:, c * CW:(c + 1) * CW])
        for j in range(NUM_STEPS):
            hid_buf[c, j, own] = done[BLK * j:BLK * j + BLK]
        g_copy(c, 1).start()
        g_copy(c, 0).start()
    for c in range(NCH):
        g_copy(c, 1).wait_recv()
        g_copy(c, 2).start()

    for d in range(3):
        st_copy(d).wait_recv()
    st_ref[1] = st_buf[...]

    @pl.when(k == 3)
    def _():
        for n, which, layer in ((0, 1, 0), (1, 0, 1), (2, 1, 1)):
            for src in range(3):
                piece = row_buf.at[which, layer, :, src * BLK:src * BLK + BLK]
                pltpu.make_async_remote_copy(
                    src_ref=piece, dst_ref=piece, send_sem=row_ssem.at[n], recv_sem=row_rsem.at[n, src],
                    device_id={"sp": 3}, device_id_type=MESH).wait_recv()
        rows_ref[...] = row_buf[...]

    for c in range(NCH):
        g_copy(c, 0).wait_recv()
        g_copy(c, 2).wait_recv()
        for j in range(NUM_STEPS):
            hid_ref[j, :, c * CW:(c + 1) * CW] = hid_buf[c, j]

    for c in range(NCH):
        for n in range(4):
            x_copy(n, c).wait_send()
        for hop in range(3):
            g_copy(c, hop).wait_send()
    for d in range(3):
        st_copy(d).wait_send()

    @pl.when(k < 3)
    def _():
        for n, which, layer in ((0, 1, 0), (1, 0, 1), (2, 1, 1)):
            row_copy(n, which, layer).wait_send()
        for layer in range(NUM_LAYERS):
            for f in range(2):
                for d in range(3):
                    rs_copy(layer, f, d).wait_send()


def layer_call(part, step_emb, state, b_in, taps, lags, gain, b_out, w_in, w_out, w_up, w_down):
    vm = pl.BlockSpec(memory_space=pltpu.VMEM)
    hbm = pl.BlockSpec(memory_space=pl.ANY)
    dma = pltpu.SemaphoreType.DMA
    return pl.pallas_call(
        layer_kernel,
        out_shape=(
            jax.ShapeDtypeStruct((NUM_STEPS, SEQ, DIM), F32),
            jax.ShapeDtypeStruct((NUM_LAYERS, 2, 3, SEQ, CH), F32),
            jax.ShapeDtypeStruct((2, NUM_LAYERS, NUM_STEPS, SEQ, CH), F32),
        ),
        in_specs=[vm] * 8 + [hbm] * 4,
        out_specs=[vm] * 3,
        scratch_shapes=[
            pltpu.VMEM(w_in.shape, BF16),
            pltpu.VMEM(w_out.shape, BF16),
            pltpu.VMEM(w_up.shape, BF16),
            pltpu.VMEM(w_down.shape, BF16),
            pltpu.VMEM((NUM_STEPS, SEQ, DIM), F32),
            pltpu.VMEM((3, NUM_STEPS, SEQ, CH), F32),
            pltpu.VMEM((3, NUM_LAYERS, 2, NUM_STEPS, BLK, CH), F32),
            pltpu.VMEM((4, NCH, NUM_STEPS * BLK, CW), F32),
            pltpu.VMEM((4, NCH, NUM_STEPS * BLK, CW), F32),
            pltpu.VMEM((NCH, NUM_STEPS, SEQ, CW), F32),
            pltpu.VMEM((2, 3, SEQ, CH), F32),
            pltpu.VMEM((2, NUM_LAYERS, NUM_STEPS, SEQ, CH), F32),
            dma((NUM_LAYERS, 4)),
            dma((NUM_LAYERS, 2, 3)),
            dma((NUM_LAYERS, 2, 3)),
            dma((4, NCH)),
            dma((4, NCH)),
            dma((3,)),
            dma((3,)),
            dma((3,)),
            dma((3, 4)),
            dma((NCH, 3)),
            dma((NCH, 3)),
        ],
        compiler_params=pltpu.CompilerParams(collective_id=0, has_side_effects=True, vmem_limit_bytes=56 << 20),
        name="layers",
    )(part, step_emb, state, b_in, taps, lags, gain, b_out, w_in, w_out, w_up, w_down)


def put_kernel(rows_ref, v_in, z_in, v_out, z_out, wide, tile, sems):
    @pl.when(lax.axis_index("sp") == 3)
    def _():
        wide[...] = jnp.zeros_like(wide)
        copies = []
        for which, dst in enumerate((v_out, z_out)):
            for layer in range(NUM_LAYERS):
                for j in range(NUM_STEPS):
                    wide[which, layer, :, j, :] = rows_ref[which, layer, j]
                tile[which, layer] = wide[which, layer].astype(BF16)
                copy = pltpu.make_async_copy(tile.at[which, layer], dst.at[layer, :, 0:8, :], sems.at[which, layer])
                copy.start()
                copies.append(copy)
        for copy in copies:
            copy.wait()


def put_call(rows, v_new, z_new):
    hbm = pl.BlockSpec(memory_space=pl.ANY)
    return pl.pallas_call(
        put_kernel,
        out_shape=(jax.ShapeDtypeStruct(v_new.shape, BF16), jax.ShapeDtypeStruct(z_new.shape, BF16)),
        in_specs=[pl.BlockSpec(memory_space=pltpu.VMEM), hbm, hbm],
        out_specs=[hbm, hbm],
        scratch_shapes=[
            pltpu.VMEM((2, NUM_LAYERS, SEQ, 8, CH), F32),
            pltpu.VMEM((2, NUM_LAYERS, SEQ, 8, CH), BF16),
            pltpu.SemaphoreType.DMA((2, NUM_LAYERS)),
        ],
        input_output_aliases={1: 0, 2: 1},
        compiler_params=pltpu.CompilerParams(vmem_limit_bytes=16 << 20),
        name="put_rows",
    )(rows, v_new, z_new)


def solution(mesh):
    def device_fn(step_emb, v_cache, z_cache, short_state, w_in, b_in, short_taps, long_filt, skip_gain, w_out, b_out, w_up, w_down):
        shard = lax.axis_index("sp").astype(jnp.int32).reshape(1)
        v_new, z_new, part = conv_call(shard, v_cache, z_cache, long_filt)
        state = jnp.transpose(short_state, (0, 2, 3, 1, 4)).astype(F32)
        hidden, states, rows = layer_call(
            part, step_emb, state, b_in, short_taps, long_filt[:, :, :8], skip_gain, b_out,
            jnp.transpose(w_in, (0, 2, 1, 3)), w_out, w_up, w_down)
        v_new, z_new = put_call(rows, v_new, z_new)
        return hidden, v_new, z_new, jnp.transpose(states, (0, 3, 1, 2, 4)).astype(BF16)

    specs_in = (
        P(None, "dp", None),
        P(None, "dp", "sp", "tp"),
        P(None, "dp", "sp", "tp"),
        P(None, "dp", None, None, "tp"),
        P(None, None, None, "tp"),
        P(None, None, "tp"),
        P(None, None, None, "tp"),
        P(None, None, None, "tp"),
        P(None, None, "tp"),
        P(None, "tp", None),
        P(None, None),
        P(None, None, "tp"),
        P(None, "tp", None),
    )
    specs_out = (
        P(None, "dp", None),
        P(None, "dp", "sp", "tp"),
        P(None, "dp", "sp", "tp"),
        P(None, "dp", None, None, "tp"),
    )
    return jax.shard_map(device_fn, mesh=mesh, in_specs=specs_in, out_specs=specs_out, check_vma=False)
```

time: 756 us -> 91.6 us (0.12); the launches traced: 746 us -> 91.2 us
  waiting for transfers between devices: 383 us -> 0 us
  other arithmetic: 151 us -> 2.04 us
  local copies, waits for them, and re-layouts: 108 us -> 8.44 us
  matrix products: 87.5 us -> 0 us
  Pallas kernels: 0 us -> 80.1 us
  between operations: 15.3 us -> 0.68 us
    psum x20 -> x0, waiting for transfers between devices: 382 us -> none  [the longest x5 129 us: device_fn(): lax.psum(part_two, 'sp')]
    reduce_sum x39 -> x0, other arithmetic: 118 us -> none  [the longest x8 49.2 us: device_fn(): jnp.sum(z_all[layer_idx] * windows[layer_idx, 1, win_start:win_start + sh...]
    dot_general x24 -> x0, matrix products: 87.5 us -> none  [the longest x8 46 us: device_fn(): jnp.dot(inner_act, w_down[layer_idx], preferred_element_type=jnp.float32)]
    pallas_call x0 -> x3, Pallas kernels: none -> 80.1 us  [the longest x1 41.1 us: layer_call(): pl.pallas_call(layer_kernel, out_shape=(jax.ShapeDtypeStruct((NUM_STEPS,...]
    unnamed x127 -> x10, local copies, waits for them, and re-layouts: 85.8 us -> 6.96 us
    dynamic_update_slice x16 -> x0, other arithmetic: 23.5 us -> none  [append_row(): lax.dynamic_update_slice(cache_all, put_row, (layer_idx, 0, row_slot, 0))]
    gather x1 -> x0, local copies, waits for them, and re-layouts: 13.7 us -> none  [filter_windows(): picked = jnp.take(long_filt, jnp.maximum(lag_pos, 0), axis=2)]
  transfers between devices with their start and end apart: 20 -> 0, of which waited for: 19 -> 0; matrix products, arithmetic and copies ran while one was open for 10% -> 0% of each run, Pallas kernels for 0% -> 0%
where the time goes in v1:
time: 91.6 us; the launch traced here: 91.2 us
  Pallas kernels  80.1 us (87%)
  local copies, waits for them, and re-layouts  8.44 us (9%)
  other arithmetic  2.04 us (2%)
    pallas_call x1, Pallas kernels, layer_call(): pl.pallas_call(layer_kernel, out_shape=(jax.ShapeDtypeStruct((NUM_STEPS,...  41.1 us
    pallas_call x1, Pallas kernels, conv_call(): pl.pallas_call(conv_kernel, out_shape=(jax.ShapeDtypeStruct(v_cache.shape...  38.9 us
    unnamed x10, local copies, waits for them, and re-layouts  6.96 us
    convert_element_type x1, other arithmetic, device_fn(): state = jnp.transpose(short_state, (0, 2, 3, 1, 4)).astype(F32)  1.99 us

profile of v1, /device:TPU:0, one launch (start us, length us, event | category | flops | bytes accessed | tf_op | source)
XLA Modules:
  0.0 91.2 jit_solution(271911609149544300)
XLA Ops:
  0.6 1.3 %copy.20.b_in_ref = f32[2,3,512]{2,1,0:T(4,128)} copy(f32[2,3,512]{2,0,1:T(2,128)} %param.18) | data formatting | bytes 24576 | tf_op args[5]
  1.9 1.4 %copy.21.taps_ref = f32[2,3,3,512]{3,2,1,0:T(4,128)} copy(f32[2,3,3,512]{3,0,2,1:T(2,128)} %param.19) | data formatting | bytes 73728 | tf_op args[6]
  3.3 1.5 %slice.3.lag_ref = f32[2,2,8,512]{3,2,1,0:T(8,128)} slice(f32[2,2,1024,512]{3,2,1,0:T(8,128)} %tail_ref.1), slice={[0:2], [0:2], [0:8], [0:512]} | slice | bytes 131072 | tf_op jit(solution)/shard_map/slice | solution.py:424
  4.8 2.0 %convert_bitcast_fusion.state_ref = f32[2,2,3,32,512]{4,3,2,1,0:T(8,128)} fusion(bf16[2,32,2,3,512]{4,2,3,1,0:T(2,128)(2,1)} %param.16), kind=kLoop, calls=%fused_computation | loop fusion | flops 196608 | bytes 1179648 | tf_op jit(solution)/shard_map/convert_element_type | solution.py:422
  6.8 38.9 %conv_stream.1 = (bf16[2,32,256,512]{3,2,1,0:T(8,128)(2,1)}, bf16[2,32,256,512]{3,2,1,0:T(8,128)(2,1)}, f32[4,2,2,4,8,512]{5,4,3,2,1,0:T(8,128)}) custom-call(s32[1]{0:T(128)} %bitcast.shard_ref, bf16[2,32,256,512]{3,2,1,0:T(8,128)(2,1)} %v_ref.1, bf16[2,32,256,512]{3,2,1,0:T(8,128)(2,1)} %z_ref.1, f32[2,2,1024,512]{3,2,1,0:T(8,128)} %tail_ref.1, ...), custom_call_target="tpu_custom_call" | custom-call | tf_op jit(solution)/shard_map/conv_stream/pallas_call | solution.py:82
  45.7 41.1 %layers.1 = (f32[4,32,1024]{2,1,0:T(8,128)}, f32[2,2,3,32,512]{4,3,2,1,0:T(8,128)}, f32[2,2,4,32,512]{4,3,2,1,0:T(8,128)}) custom-call(f32[4,2,2,4,8,512]{5,4,3,2,1,0:T(8,128)} %get-tuple-element.12.part_ref, bf16[4,32,1024]{2,1,0:T(8,128)(2,1)} %emb_ref.1, f32[2,2,3,32,512]{4,3,2,1,0:T(8,128)} %convert_bitcast_fusion.state_ref, ...), custom_call_target="tpu_custom_call" | custom-call | tf_op jit(solution)/shard_map/layers/pallas_call | solution.py:344
  86.9 0.0 copy-start
  86.9 1.2 %copy-done = f32[2,2,4,32,512]{4,3,2,1,0:T(8,128)S(1)} copy-done((f32[2,2,4,32,512]{4,3,2,1,0:T(8,128)S(1)}, f32[2,2,4,32,512]{4,3,2,1,0:T(8,128)}, u32[]{:S(2)}) %copy-start) | copy-done | bytes 1048600
  88.1 0.0 copy-start.1
  88.1 0.0 copy-start.2
  88.1 1.1 %copy-done.1 = f32[2,2,3,32,512]{4,3,2,1,0:T(8,128)S(1)} copy-done((f32[2,2,3,32,512]{4,3,2,1,0:T(8,128)S(1)}, f32[2,2,3,32,512]{4,3,2,1,0:T(8,128)}, u32[]{:S(2)}) %copy-start.1) | copy-done | bytes 786456
  89.2 0.1 convert_bitcast_fusion.1
  89.3 1.2 %copy.22 = bf16[2,32,2,3,512]{4,2,3,1,0:T(2,128)(2,1)} copy(bf16[2,32,2,3,512]{4,1,3,2,0:T(8,128)(2,1)S(1)} %convert_bitcast_fusion.1) | data formatting | bytes 786432
  90.4 0.0 copy-done.2
  90.4 0.8 copy.27
  (1 shorter events, 0.0 us)
Async XLA Ops:
  86.9 1.2 %copy-start = (f32[2,2,4,32,512]{4,3,2,1,0:T(8,128)S(1)}, f32[2,2,4,32,512]{4,3,2,1,0:T(8,128)}, u32[]{:S(2)}) copy-start(f32[2,2,4,32,512]{4,3,2,1,0:T(8,128)} %get-tuple-element.14.rows_ref) | copy-start | bytes 3145732
  88.1 1.1 %copy-start.1 = (f32[2,2,3,32,512]{4,3,2,1,0:T(8,128)S(1)}, f32[2,2,3,32,512]{4,3,2,1,0:T(8,128)}, u32[]{:S(2)}) copy-start(f32[2,2,3,32,512]{4,3,2,1,0:T(8,128)} %get-tuple-element.19) | copy-start | bytes 2359300
  88.1 2.3 %copy-start.2 = (f32[4,32,1024]{2,1,0:T(8,128)S(1)}, f32[4,32,1024]{2,1,0:T(8,128)}, u32[]{:S(2)}) copy-start(f32[4,32,1024]{2,1,0:T(8,128)} %get-tuple-element.28) | copy-start | bytes 1572868
